TPU v7x, 32 devices: a whole 2x2x4 slice. The times are simulated.
32 devices in a mesh: group: 4 (over y, core), sub: 8 (over z, x).
Axes of the slice: x: 2, y: 2, z: 4, core: 2. Of those that a mesh axis runs over, the one named last changes fastest.
Arguments:
- shared_sizes: int32 [4, 8, 2], P('group', 'sub'), may hold values from 0 to 256, as said below
- stiffness: float32 [4, 8], P('group', 'sub'), may hold values from 0.1 to 10
- load_cases: float32 [4, 8, 1024, 384], P('group', 'sub'), may hold values from -6 to 6
- schur_blocks: bfloat16 [4, 8, 1024, 1024], P('group', 'sub')
- neumann_inverse: bfloat16 [4, 8, 1024, 1024], P('group', 'sub')
- coarse_basis: bfloat16 [4, 8, 32, 1024], P('group', 'sub'), may hold values from -0.1875 to 0.1875
- coarse_dofs: int32 [4, 8, 32], P('group', 'sub'), may hold values from 0 to 511
- coarse_inverse: float32 [512, 512], P('sub'), as said below
Outputs:
- solution: float32 [4, 8, 1024, 384], P('group', 'sub')
- residual: float32 [4, 8, 1024, 384], P('group', 'sub')
Inputs may be any that keep to these rules, and one draw needn't show every extreme that they name: shared_sizes[g, s, 0] equals shared_sizes[g, s - 1, 1]; the lower share of the first and the upper share of the last subdomain of a group are 0, the other shares lie in 128 to 256, and in every group some subdomain shares exactly 256 with its upper neighbour. `coarse_inverse`: symmetric.
All inputs are finite; a program needn't handle non-finite values.
Results may differ from a plain program's by a relative error of at most 0.0075.
Values sent between devices are 32-bit elements; how exact they have to be, the bound alone decides.
No kernel may reach another device: no remote copies, remote signals or barrier semaphores. Data moves between devices by JAX's collectives and lax.ppermute only.
A program may use at most 128 MiB of HBM per device.

v0:
```python
import jax
import jax.numpy as jnp
from jax import lax
from jax.sharding import PartitionSpec as P

MAXSH = 256
ITERS = 4
OMEGA = 0.6


def from_behind(block, axis, distance):
    devices = range(lax.axis_size(axis))
    route = [(i - distance, i) for i in devices if i - distance in devices]
    return lax.ppermute(block, axis, route)


def extended(x, sides, width):
    for axis, dim in sides:
        peers, length = (lax.axis_size(axis), x.shape[dim])
        up = [(i, (i + 1) % peers) for i in range(peers - 1)]
        down = [(j, i) for i, j in up]
        last = lax.slice_in_dim(x, length - width, length, axis=dim)
        leading = lax.slice_in_dim(x, 0, width, axis=dim)
        before = lax.ppermute(last, axis, up)
        after = lax.ppermute(leading, axis, down)
        x = jnp.concatenate([before, x, after], axis=dim)
    return x


def lift_piece(tail_rows, share_size):
    slab_width = tail_rows.shape[0]
    rolled = jnp.roll(tail_rows, share_size - slab_width, axis=0)
    inside = (jnp.arange(slab_width) < share_size)[:, None]
    return jnp.where(inside, rolled, jnp.zeros_like(rolled))


def place_piece(head_rows, share_size):
    slab_width = head_rows.shape[0]
    inside = (jnp.arange(slab_width) < share_size)[:, None]
    masked = jnp.where(inside, head_rows, jnp.zeros_like(head_rows))
    return jnp.roll(masked, slab_width - share_size, axis=0)


def assemble(vector, share_up):
    unknowns = vector.shape[0]
    tail_rows = vector[unknowns - MAXSH :]
    head_rows = vector[:MAXSH]
    lifted = lift_piece(tail_rows, share_up)
    from_lower = from_behind(lifted, "sub", 1)
    from_upper = from_behind(head_rows, "sub", -1)
    placed = place_piece(from_upper, share_up)
    return jnp.concatenate(
        [head_rows + from_lower, vector[MAXSH : unknowns - MAXSH], tail_rows + placed], axis=0
    )


def on_device(
    shared_sizes,
    stiffness,
    load_cases,
    schur_blocks,
    neumann_inverse,
    coarse_basis,
    coarse_dofs,
    coarse_inverse,
):
    share_low = shared_sizes[0, 0, 0]
    share_up = shared_sizes[0, 0, 1]
    beside_all = extended(stiffness, (("sub", 1),), 1)
    own_stiff = beside_all[0, 1]
    low_weight = own_stiff / (own_stiff + beside_all[0, 0])
    up_weight = own_stiff / (own_stiff + beside_all[0, 2])
    loads = load_cases[0, 0]
    schur = schur_blocks[0, 0]
    neumann = neumann_inverse[0, 0]
    basis = coarse_basis[0, 0]
    my_dofs = coarse_dofs[0, 0]
    unknowns, cases = loads.shape
    own_count = coarse_inverse.shape[0]
    row_index = jnp.arange(unknowns)
    weight = jnp.where(
        row_index < share_low,
        low_weight,
        jnp.where(row_index >= unknowns - share_up, up_weight, jnp.float32(1.0)),
    )[:, None]
    highest = lax.Precision.HIGHEST

    def operator_residual(solution):
        return loads - jnp.dot(
            schur, solution.astype(jnp.bfloat16), preferred_element_type=jnp.float32
        )

    solution = jnp.zeros((unknowns, cases), jnp.float32)
    for sweep in range(ITERS):
        local = operator_residual(solution)
        weighted = (weight * assemble(local, share_up)).astype(jnp.bfloat16)
        coarse_terms = jnp.dot(basis, weighted, preferred_element_type=jnp.float32)
        dof_values = my_dofs.astype(jnp.float32)
        all_terms = lax.all_gather(coarse_terms, "sub", axis=0, tiled=True)
        all_dofs = lax.all_gather(dof_values, "sub", axis=0, tiled=True)
        dof_index = all_dofs.astype(jnp.int32)
        first_row = lax.axis_index("sub") * own_count
        own_select = (dof_index[:, None] == first_row + jnp.arange(own_count)[None, :]).astype(
            jnp.float32
        )
        owned = lax.dot_general(own_select, all_terms, (((0,), (0,)), ((), ())), precision=highest)
        owned = lax.psum(owned, "group")
        columns = jnp.take(coarse_inverse, dof_index, axis=1)
        partial_vals = lax.dot_general(columns, owned, (((0,), (0,)), ((), ())), precision=highest)
        partial_vals = partial_vals.reshape(-1, coarse_terms.shape[0], cases)
        received = lax.all_to_all(partial_vals, "sub", split_axis=0, concat_axis=0, tiled=True)
        picked = jnp.sum(received, axis=0)
        picked = picked.astype(jnp.bfloat16)
        correction = jnp.dot(neumann, weighted, preferred_element_type=jnp.float32)
        correction = correction + lax.dot_general(
            basis, picked, (((0,), (0,)), ((), ())), preferred_element_type=jnp.float32
        )
        solution = solution + OMEGA * assemble(weight * correction, share_up)
    residual = assemble(operator_residual(solution), share_up)
    return (solution[None, None], residual[None, None])


def solution(mesh):
    return jax.shard_map(
        on_device,
        mesh=mesh,
        in_specs=(
            P("group", "sub", None),
            P("group", "sub"),
            P("group", "sub", None, None),
            P("group", "sub", None, None),
            P("group", "sub", None, None),
            P("group", "sub", None, None),
            P("group", "sub", None),
            P("sub", None),
        ),
        out_specs=(P("group", "sub", None, None), P("group", "sub", None, None)),
        check_vma=False,
    )
```

profile of v0, /device:TPU:16, one launch (start us, length us, event | category | flops | bytes accessed | tf_op | source)
XLA Modules:
  0.0 597.5 jit_solution(9661922671992732006)
XLA Ops:
  7.2 3.4 collective-permute-start.1
  13.2 3.0 copy.14
  20.8 4.2 collective-permute-start.3
  31.0 14.9 %all-reduce = f32[256]{0:T(256)S(1)} all-reduce(f32[256]{0:T(256)S(1)} %bitcast_dynamic-update-slice_fusion), channel_id=2, replica_groups=mesh['group'=4,'sub'=8] {'sub'}, use_global_device_ids=true, to_apply=%add | all-reduce | flops 256 | bytes 2048
  49.6 2.8 collective-permute-start.2
  54.6 6.0 %collective-permute-done.2 = f32[256,384]{0,1:T(8,128)} collective-permute-done((f32[256,384]{0,1:T(8,128)}, f32[256,384]{0,1:T(8,128)}, u32[]{:S(2)}, u32[]{:S(2)}) %collective-permute-start.2) | collective-permute-done | bytes 393248 | tf_op jit(solution)/shard_map/ppermute | solution.py:14
  63.2 27.9 %all_gather.19 = f32[256,384]{1,0:T(8,128)S(1)} all-gather(f32[32,384]{1,0:T(8,128)S(1)} %convolution_bitcast_fusion.3), channel_id=1, replica_groups=mesh['group'=4,'sub'=8] {'sub'}, dimensions={0}, use_global_device_ids=true | all-gather | bytes 442368 | tf_op jit(solution)/shard_map/all_gather | solution.py:99
  93.1 34.8 %all-reduce.6.cloned.1.call-done = f32[64,384]{1,0:T(8,128)} async-done(((f32[64,384]{1,0:T(8,128)}), f32[64,384]{1,0:T(8,128)}) %all-reduce.6.cloned.1.call-update) | async-done | bytes 98320 | tf_op jit(solution)/shard_map/psum | solution.py:107
  129.4 15.0 %all_to_all.20 = f32[8,32,384]{2,1,0:T(8,128)} all-to-all(f32[8,32,384]{2,1,0:T(8,128)S(1)} %bitcast.145), channel_id=1, replica_groups=mesh['group'=4,'sub'=8] {'sub'}, dimensions={0} | all-to-all | bytes 786432 | tf_op jit(solution)/shard_map/all_to_all | solution.py:111
  146.4 2.6 multiply_bitcast_fusion.3
  149.1 3.2 collective-permute-start.5
  152.3 8.6 %collective-permute-done.5 = f32[256,384]{0,1:T(8,128)S(1)} collective-permute-done((f32[256,384]{0,1:T(8,128)S(1)}, f32[256,384]{0,1:T(8,128)S(1)}, u32[]{:S(2)}, u32[]{:S(2)}) %collective-permute-start.5) | collective-permute-done | bytes 393248 | tf_op jit(solution)/shard_map/ppermute | solution.py:14
  161.2 3.0 collective-permute-start.4
  165.2 7.9 %collective-permute-done.4 = f32[256,384]{0,1:T(8,128)S(1)} collective-permute-done((f32[256,384]{0,1:T(8,128)S(1)}, f32[256,384]{0,1:T(8,128)S(1)}, u32[]{:S(2)}, u32[]{:S(2)}) %collective-permute-start.4) | collective-permute-done | bytes 393248 | tf_op jit(solution)/shard_map/ppermute | solution.py:14
  176.5 8.2 %collective-permute-done.7 = f32[256,384]{0,1:T(8,128)S(1)} collective-permute-done((f32[256,384]{0,1:T(8,128)S(1)}, f32[256,384]{0,1:T(8,128)S(1)}, u32[]{:S(2)}, u32[]{:S(2)}) %collective-permute-start.7) | collective-permute-done | bytes 393248 | tf_op jit(solution)/shard_map/ppermute | solution.py:14
  187.6 8.1 %collective-permute-done.6 = f32[256,384]{0,1:T(8,128)S(1)} collective-permute-done((f32[256,384]{0,1:T(8,128)S(1)}, f32[256,384]{0,1:T(8,128)S(1)}, u32[]{:S(2)}, u32[]{:S(2)}) %collective-permute-start.6) | collective-permute-done | bytes 393248 | tf_op jit(solution)/shard_map/ppermute | solution.py:14
  196.3 25.4 %all_gather.20 = f32[256,384]{1,0:T(8,128)S(1)} all-gather(f32[32,384]{1,0:T(8,128)S(1)} %convolution_bitcast_fusion.2), channel_id=1, replica_groups=mesh['group'=4,'sub'=8] {'sub'}, dimensions={0}, use_global_device_ids=true | all-gather | bytes 442368 | tf_op jit(solution)/shard_map/all_gather | solution.py:99
  222.8 34.4 %all-reduce.8.cloned.1.call-done = f32[64,384]{1,0:T(8,128)} async-done(((f32[64,384]{1,0:T(8,128)}), f32[64,384]{1,0:T(8,128)}) %all-reduce.8.cloned.1.call-update) | async-done | bytes 98320 | tf_op jit(solution)/shard_map/psum | solution.py:107
  258.6 14.9 %all_to_all.21 = f32[8,32,384]{2,1,0:T(8,128)} all-to-all(f32[8,32,384]{2,1,0:T(8,128)S(1)} %bitcast.146), channel_id=1, replica_groups=mesh['group'=4,'sub'=8] {'sub'}, dimensions={0} | all-to-all | bytes 786432 | tf_op jit(solution)/shard_map/all_to_all | solution.py:111
  275.7 2.6 multiply_bitcast_fusion.2
  278.5 3.2 collective-permute-start.9
  281.7 8.6 %collective-permute-done.9 = f32[256,384]{0,1:T(8,128)S(1)} collective-permute-done((f32[256,384]{0,1:T(8,128)S(1)}, f32[256,384]{0,1:T(8,128)S(1)}, u32[]{:S(2)}, u32[]{:S(2)}) %collective-permute-start.9) | collective-permute-done | bytes 393248 | tf_op jit(solution)/shard_map/ppermute | solution.py:14
  290.6 3.2 collective-permute-start.8
  294.9 7.6 %collective-permute-done.8 = f32[256,384]{0,1:T(8,128)S(1)} collective-permute-done((f32[256,384]{0,1:T(8,128)S(1)}, f32[256,384]{0,1:T(8,128)S(1)}, u32[]{:S(2)}, u32[]{:S(2)}) %collective-permute-start.8) | collective-permute-done | bytes 393248 | tf_op jit(solution)/shard_map/ppermute | solution.py:14
  305.9 8.2 %collective-permute-done.11 = f32[256,384]{0,1:T(8,128)S(1)} collective-permute-done((f32[256,384]{0,1:T(8,128)S(1)}, f32[256,384]{0,1:T(8,128)S(1)}, u32[]{:S(2)}, u32[]{:S(2)}) %collective-permute-start.11) | collective-permute-done | bytes 393248 | tf_op jit(solution)/shard_map/ppermute | solution.py:14
  317.0 8.0 %collective-permute-done.10 = f32[256,384]{0,1:T(8,128)S(1)} collective-permute-done((f32[256,384]{0,1:T(8,128)S(1)}, f32[256,384]{0,1:T(8,128)S(1)}, u32[]{:S(2)}, u32[]{:S(2)}) %collective-permute-start.10) | collective-permute-done | bytes 393248 | tf_op jit(solution)/shard_map/ppermute | solution.py:14
  325.7 25.4 %all_gather.21 = f32[256,384]{1,0:T(8,128)S(1)} all-gather(f32[32,384]{1,0:T(8,128)S(1)} %convolution_bitcast_fusion.1), channel_id=1, replica_groups=mesh['group'=4,'sub'=8] {'sub'}, dimensions={0}, use_global_device_ids=true | all-gather | bytes 442368 | tf_op jit(solution)/shard_map/all_gather | solution.py:99
  352.2 34.4 %all-reduce.10.cloned.1.call-done = f32[64,384]{1,0:T(8,128)} async-done(((f32[64,384]{1,0:T(8,128)}), f32[64,384]{1,0:T(8,128)}) %all-reduce.10.cloned.1.call-update) | async-done | bytes 98320 | tf_op jit(solution)/shard_map/psum | solution.py:107
  388.0 14.9 %all_to_all.22 = f32[8,32,384]{2,1,0:T(8,128)} all-to-all(f32[8,32,384]{2,1,0:T(8,128)S(1)} %bitcast.147), channel_id=1, replica_groups=mesh['group'=4,'sub'=8] {'sub'}, dimensions={0} | all-to-all | bytes 786432 | tf_op jit(solution)/shard_map/all_to_all | solution.py:111
  405.1 2.7 multiply_bitcast_fusion.1
  407.9 3.2 collective-permute-start.13
  411.1 8.6 %collective-permute-done.13 = f32[256,384]{0,1:T(8,128)S(1)} collective-permute-done((f32[256,384]{0,1:T(8,128)S(1)}, f32[256,384]{0,1:T(8,128)S(1)}, u32[]{:S(2)}, u32[]{:S(2)}) %collective-permute-start.13) | collective-permute-done | bytes 393248 | tf_op jit(solution)/shard_map/ppermute | solution.py:14
  420.0 3.0 collective-permute-start.12
  424.0 7.9 %collective-permute-done.12 = f32[256,384]{0,1:T(8,128)S(1)} collective-permute-done((f32[256,384]{0,1:T(8,128)S(1)}, f32[256,384]{0,1:T(8,128)S(1)}, u32[]{:S(2)}, u32[]{:S(2)}) %collective-permute-start.12) | collective-permute-done | bytes 393248 | tf_op jit(solution)/shard_map/ppermute | solution.py:14
  435.4 8.2 %collective-permute-done.15 = f32[256,384]{0,1:T(8,128)S(1)} collective-permute-done((f32[256,384]{0,1:T(8,128)S(1)}, f32[256,384]{0,1:T(8,128)S(1)}, u32[]{:S(2)}, u32[]{:S(2)}) %collective-permute-start.15) | collective-permute-done | bytes 393248 | tf_op jit(solution)/shard_map/ppermute | solution.py:14
  446.5 8.1 %collective-permute-done.14 = f32[256,384]{0,1:T(8,128)S(1)} collective-permute-done((f32[256,384]{0,1:T(8,128)S(1)}, f32[256,384]{0,1:T(8,128)S(1)}, u32[]{:S(2)}, u32[]{:S(2)}) %collective-permute-start.14) | collective-permute-done | bytes 393248 | tf_op jit(solution)/shard_map/ppermute | solution.py:14
  455.2 25.4 %all_gather.22 = f32[256,384]{1,0:T(8,128)S(1)} all-gather(f32[32,384]{1,0:T(8,128)S(1)} %convolution_bitcast_fusion), channel_id=1, replica_groups=mesh['group'=4,'sub'=8] {'sub'}, dimensions={0}, use_global_device_ids=true | all-gather | bytes 442368 | tf_op jit(solution)/shard_map/all_gather | solution.py:99
  481.6 34.4 %all-reduce.12.cloned.1.call-done = f32[64,384]{1,0:T(8,128)} async-done(((f32[64,384]{1,0:T(8,128)}), f32[64,384]{1,0:T(8,128)}) %all-reduce.12.cloned.1.call-update) | async-done | bytes 98320 | tf_op jit(solution)/shard_map/psum | solution.py:107
  517.5 14.9 %all_to_all.23 = f32[8,32,384]{2,1,0:T(8,128)} all-to-all(f32[8,32,384]{2,1,0:T(8,128)S(1)} %bitcast.144), channel_id=1, replica_groups=mesh['group'=4,'sub'=8] {'sub'}, dimensions={0} | all-to-all | bytes 786432 | tf_op jit(solution)/shard_map/all_to_all | solution.py:111
  534.6 2.7 multiply_bitcast_fusion
  537.3 3.2 collective-permute-start.17
  540.6 8.6 %collective-permute-done.17 = f32[256,384]{0,1:T(8,128)S(1)} collective-permute-done((f32[256,384]{0,1:T(8,128)S(1)}, f32[256,384]{0,1:T(8,128)S(1)}, u32[]{:S(2)}, u32[]{:S(2)}) %collective-permute-start.17) | collective-permute-done | bytes 393248 | tf_op jit(solution)/shard_map/ppermute | solution.py:14
  549.5 3.0 collective-permute-start.16
  552.6 8.7 %collective-permute-done.16 = f32[256,384]{0,1:T(8,128)S(1)} collective-permute-done((f32[256,384]{0,1:T(8,128)S(1)}, f32[256,384]{0,1:T(8,128)S(1)}, u32[]{:S(2)}, u32[]{:S(2)}) %collective-permute-start.16) | collective-permute-done | bytes 393248 | tf_op jit(solution)/shard_map/ppermute | solution.py:14
  565.0 8.2 %collective-permute-done.19 = f32[256,384]{0,1:T(8,128)S(1)} collective-permute-done((f32[256,384]{0,1:T(8,128)S(1)}, f32[256,384]{0,1:T(8,128)S(1)}, u32[]{:S(2)}, u32[]{:S(2)}) %collective-permute-start.19) | collective-permute-done | bytes 393248 | tf_op jit(solution)/shard_map/ppermute | solution.py:14
  578.5 3.0 copy.16
  581.5 3.6 collective-permute-done.18
  588.0 3.0 copy.17
  (199 shorter events, 72.9 us)
Async XLA Ops:
  7.2 9.1 %copy-start = (bf16[1,1,1024,1024]{3,2,1,0:T(8,128)(2,1)S(1)}, bf16[1,1,1024,1024]{3,2,1,0:T(8,128)(2,1)}, u32[]{:S(2)}) copy-start(bf16[1,1,1024,1024]{3,2,1,0:T(8,128)(2,1)} %param.15) | copy-start | bytes 6291460
  7.2 120.8 %all-reduce.6.cloned.1.call-start = ((), (), s32[]{:S(2)}) async-start(), calls=%async_computation.4 | async-start | bytes 196608 | tf_op jit(solution)/shard_map/psum | solution.py:107
  7.2 45.2 %collective-permute-start.1 = (f32[1,1]{1,0:T(1,128)}, f32[1,1]{1,0:T(1,128)}, u32[]{:S(2)}, u32[]{:S(2)}) collective-permute-start(f32[1,1]{1,0:T(1,128)} %param.13), channel_id=1, source_target_pairs={{1,0},{2,1},{3,2},{4,3},{5,4},{6,5},{7,6},{9,8},{10,9},{11,10},{12... | collective-permute-start | bytes 20 | tf_op jit(solution)/shard_map/ppermute | solution.py:25
  10.7 42.5 %collective-permute-start = (f32[1,1]{1,0:T(1,128)}, f32[1,1]{1,0:T(1,128)}, u32[]{:S(2)}, u32[]{:S(2)}) collective-permute-start(f32[1,1]{1,0:T(1,128)} %param.13), channel_id=1, source_target_pairs={{0,1},{1,2},{2,3},{3,4},{4,5},{5,6},{6,7},{8,9},{9,10},{10,11},{11... | collective-permute-start | bytes 20 | tf_op jit(solution)/shard_map/ppermute | solution.py:24
  20.8 25.8 %collective-permute-start.3 = (f32[256,384]{0,1:T(8,128)}, f32[256,384]{0,1:T(8,128)S(1)}, u32[]{:S(2)}, u32[]{:S(2)}) collective-permute-start(f32[256,384]{0,1:T(8,128)} %get-tuple-element.51), channel_id=1, source_target_pairs={{1,0},{2,1},{3,2},{4,3},{5,4},{6,5},{7,6},{9,8},{10,9},{11,10},{12... | collective-permute-start | bytes 1179656 | tf_op jit(solution)/shard_map/ppermute | solution.py:14
  49.6 13.3 %copy-start.40 = (bf16[1,1,32,1024]{3,2,1,0:T(8,128)(2,1)S(1)}, bf16[1,1,32,1024]{3,2,1,0:T(8,128)(2,1)}, u32[]{:S(2)}) copy-start(bf16[1,1,32,1024]{3,2,1,0:T(8,128)(2,1)} %param.17) | copy-start | bytes 196612
  49.6 11.0 %collective-permute-start.2 = (f32[256,384]{0,1:T(8,128)}, f32[256,384]{0,1:T(8,128)}, u32[]{:S(2)}, u32[]{:S(2)}) collective-permute-start(f32[256,384]{0,1:T(8,128)} %get-tuple-element.70), channel_id=1, source_target_pairs={{0,1},{1,2},{2,3},{3,4},{4,5},{5,6},{6,7},{8,9},{9,10},{10,11},{11... | collective-permute-start | bytes 1179656 | tf_op jit(solution)/shard_map/ppermute | solution.py:14
  62.8 29.4 %copy-start.47 = (f32[64,512]{1,0:T(8,128)S(1)}, f32[64,512]{1,0:T(8,128)}, u32[]{:S(2)}) copy-start(f32[64,512]{1,0:T(8,128)} %param.19) | copy-start | bytes 393220
  92.2 165.0 %all-reduce.8.cloned.1.call-start = ((), (), s32[]{:S(2)}) async-start(), calls=%async_computation.5 | async-start | bytes 196608 | tf_op jit(solution)/shard_map/psum | solution.py:107
  129.4 16.4 %copy-start.21 = (f32[256,384]{0,1:T(8,128)S(1)}, f32[256,384]{0,1:T(8,128)}, u32[]{:S(2)}) copy-start(f32[256,384]{0,1:T(8,128)} %copy-done.20) | copy-start | bytes 1179652
  149.1 11.8 %collective-permute-start.5 = (f32[256,384]{0,1:T(8,128)S(1)}, f32[256,384]{0,1:T(8,128)S(1)}, u32[]{:S(2)}, u32[]{:S(2)}) collective-permute-start(f32[256,384]{0,1:T(8,128)S(1)} %get-tuple-element.47), channel_id=1, source_target_pairs={{1,0},{2,1},{3,2},{4,3},{5,4},{6,5},{7,6},{9,8},{10,9},{11,10},{12... | collective-permute-start | bytes 1179656 | tf_op jit(solution)/shard_map/ppermute | solution.py:14
  161.2 11.9 %collective-permute-start.4 = (f32[256,384]{0,1:T(8,128)S(1)}, f32[256,384]{0,1:T(8,128)S(1)}, u32[]{:S(2)}, u32[]{:S(2)}) collective-permute-start(f32[256,384]{0,1:T(8,128)S(1)} %get-tuple-element.66), channel_id=1, source_target_pairs={{0,1},{1,2},{2,3},{3,4},{4,5},{5,6},{6,7},{8,9},{9,10},{10,11},{11... | collective-permute-start | bytes 1179656 | tf_op jit(solution)/shard_map/ppermute | solution.py:14
  165.2 9.3 %copy-start.13 = (f32[512,384]{0,1:T(8,128)}, f32[512,384]{0,1:T(8,128)S(1)}, u32[]{:S(2)}) copy-start(f32[512,384]{0,1:T(8,128)S(1)} %get-tuple-element.42) | copy-start | bytes 2359300
  174.6 10.1 %collective-permute-start.7 = (f32[256,384]{0,1:T(8,128)S(1)}, f32[256,384]{0,1:T(8,128)S(1)}, u32[]{:S(2)}, u32[]{:S(2)}) collective-permute-start(f32[256,384]{0,1:T(8,128)S(1)} %get-tuple-element.41), channel_id=1, source_target_pairs={{1,0},{2,1},{3,2},{4,3},{5,4},{6,5},{7,6},{9,8},{10,9},{11,10},{12... | collective-permute-start | bytes 1179656 | tf_op jit(solution)/shard_map/ppermute | solution.py:14
  185.0 10.7 %collective-permute-start.6 = (f32[256,384]{0,1:T(8,128)S(1)}, f32[256,384]{0,1:T(8,128)S(1)}, u32[]{:S(2)}, u32[]{:S(2)}) collective-permute-start(f32[256,384]{0,1:T(8,128)S(1)} %get-tuple-element.64), channel_id=1, source_target_pairs={{0,1},{1,2},{2,3},{3,4},{4,5},{5,6},{6,7},{8,9},{9,10},{10,11},{11... | collective-permute-start | bytes 1179656 | tf_op jit(solution)/shard_map/ppermute | solution.py:14
  187.6 8.7 %copy-start.9 = (f32[512,384]{0,1:T(8,128)}, f32[512,384]{0,1:T(8,128)S(1)}, u32[]{:S(2)}) copy-start(f32[512,384]{0,1:T(8,128)S(1)} %slice.126) | copy-start | bytes 2359300
  195.9 25.8 %copy-start.26 = (f32[256,384]{0,1:T(8,128)}, f32[256,384]{0,1:T(8,128)S(1)}, u32[]{:S(2)}) copy-start(f32[256,384]{0,1:T(8,128)S(1)} %get-tuple-element.39) | copy-start | bytes 1179652
  222.7 163.8 %all-reduce.10.cloned.1.call-start = ((), (), s32[]{:S(2)}) async-start(), calls=%async_computation.6 | async-start | bytes 196608 | tf_op jit(solution)/shard_map/psum | solution.py:107
  278.5 11.8 %collective-permute-start.9 = (f32[256,384]{0,1:T(8,128)S(1)}, f32[256,384]{0,1:T(8,128)S(1)}, u32[]{:S(2)}, u32[]{:S(2)}) collective-permute-start(f32[256,384]{0,1:T(8,128)S(1)} %get-tuple-element.37), channel_id=1, source_target_pairs={{1,0},{2,1},{3,2},{4,3},{5,4},{6,5},{7,6},{9,8},{10,9},{11,10},{12... | collective-permute-start | bytes 1179656 | tf_op jit(solution)/shard_map/ppermute | solution.py:14
  290.6 11.9 %collective-permute-start.8 = (f32[256,384]{0,1:T(8,128)S(1)}, f32[256,384]{0,1:T(8,128)S(1)}, u32[]{:S(2)}, u32[]{:S(2)}) collective-permute-start(f32[256,384]{0,1:T(8,128)S(1)} %get-tuple-element.62), channel_id=1, source_target_pairs={{0,1},{1,2},{2,3},{3,4},{4,5},{5,6},{6,7},{8,9},{9,10},{10,11},{11... | collective-permute-start | bytes 1179656 | tf_op jit(solution)/shard_map/ppermute | solution.py:14
  294.9 9.0 %copy-start.41 = (f32[512,384]{0,1:T(8,128)}, f32[512,384]{0,1:T(8,128)S(1)}, u32[]{:S(2)}) copy-start(f32[512,384]{0,1:T(8,128)S(1)} %get-tuple-element.32) | copy-start | bytes 2359300
  303.9 10.1 %collective-permute-start.11 = (f32[256,384]{0,1:T(8,128)S(1)}, f32[256,384]{0,1:T(8,128)S(1)}, u32[]{:S(2)}, u32[]{:S(2)}) collective-permute-start(f32[256,384]{0,1:T(8,128)S(1)} %get-tuple-element.31), channel_id=1, source_target_pairs={{1,0},{2,1},{3,2},{4,3},{5,4},{6,5},{7,6},{9,8},{10,9},{11,10},{12... | collective-permute-start | bytes 1179656 | tf_op jit(solution)/shard_map/ppermute | solution.py:14
  314.3 10.7 %collective-permute-start.10 = (f32[256,384]{0,1:T(8,128)S(1)}, f32[256,384]{0,1:T(8,128)S(1)}, u32[]{:S(2)}, u32[]{:S(2)}) collective-permute-start(f32[256,384]{0,1:T(8,128)S(1)} %get-tuple-element.60), channel_id=1, source_target_pairs={{0,1},{1,2},{2,3},{3,4},{4,5},{5,6},{6,7},{8,9},{9,10},{10,11},{11... | collective-permute-start | bytes 1179656 | tf_op jit(solution)/shard_map/ppermute | solution.py:14
  325.3 25.8 %copy-start.28 = (f32[256,384]{0,1:T(8,128)}, f32[256,384]{0,1:T(8,128)S(1)}, u32[]{:S(2)}) copy-start(f32[256,384]{0,1:T(8,128)S(1)} %get-tuple-element.29) | copy-start | bytes 1179652
  352.1 163.9 %all-reduce.12.cloned.1.call-start = ((), (), s32[]{:S(2)}) async-start(), calls=%async_computation.7 | async-start | bytes 196608 | tf_op jit(solution)/shard_map/psum | solution.py:107
  407.9 11.9 %collective-permute-start.13 = (f32[256,384]{0,1:T(8,128)S(1)}, f32[256,384]{0,1:T(8,128)S(1)}, u32[]{:S(2)}, u32[]{:S(2)}) collective-permute-start(f32[256,384]{0,1:T(8,128)S(1)} %get-tuple-element.27), channel_id=1, source_target_pairs={{1,0},{2,1},{3,2},{4,3},{5,4},{6,5},{7,6},{9,8},{10,9},{11,10},{12... | collective-permute-start | bytes 1179656 | tf_op jit(solution)/shard_map/ppermute | solution.py:14
  420.0 11.9 %collective-permute-start.12 = (f32[256,384]{0,1:T(8,128)S(1)}, f32[256,384]{0,1:T(8,128)S(1)}, u32[]{:S(2)}, u32[]{:S(2)}) collective-permute-start(f32[256,384]{0,1:T(8,128)S(1)} %get-tuple-element.58), channel_id=1, source_target_pairs={{0,1},{1,2},{2,3},{3,4},{4,5},{5,6},{6,7},{8,9},{9,10},{10,11},{11... | collective-permute-start | bytes 1179656 | tf_op jit(solution)/shard_map/ppermute | solution.py:14
  423.0 9.2 %copy-start.31 = (f32[256,384]{0,1:T(8,128)S(1)}, f32[256,384]{0,1:T(8,128)}, u32[]{:S(2)}) copy-start(f32[256,384]{0,1:T(8,128)} %copy-done.30) | copy-start | bytes 1179652
  423.0 9.2 %copy-start.34 = (f32[256,384]{0,1:T(8,128)S(1)}, f32[256,384]{0,1:T(8,128)}, u32[]{:S(2)}) copy-start(f32[256,384]{0,1:T(8,128)} %copy-done.33) | copy-start | bytes 1179652
  423.0 9.2 %copy-start.42 = (f32[512,384]{0,1:T(8,128)S(1)}, f32[512,384]{0,1:T(8,128)}, u32[]{:S(2)}) copy-start(f32[512,384]{0,1:T(8,128)} %copy-done.41) | copy-start | bytes 2359300
  424.0 9.4 %copy-start.44 = (f32[512,384]{0,1:T(8,128)}, f32[512,384]{0,1:T(8,128)S(1)}, u32[]{:S(2)}) copy-start(f32[512,384]{0,1:T(8,128)S(1)} %get-tuple-element.22) | copy-start | bytes 2359300
  433.4 10.1 %collective-permute-start.15 = (f32[256,384]{0,1:T(8,128)S(1)}, f32[256,384]{0,1:T(8,128)S(1)}, u32[]{:S(2)}, u32[]{:S(2)}) collective-permute-start(f32[256,384]{0,1:T(8,128)S(1)} %get-tuple-element.21), channel_id=1, source_target_pairs={{1,0},{2,1},{3,2},{4,3},{5,4},{6,5},{7,6},{9,8},{10,9},{11,10},{12... | collective-permute-start | bytes 1179656 | tf_op jit(solution)/shard_map/ppermute | solution.py:14
  443.9 10.7 %collective-permute-start.14 = (f32[256,384]{0,1:T(8,128)S(1)}, f32[256,384]{0,1:T(8,128)S(1)}, u32[]{:S(2)}, u32[]{:S(2)}) collective-permute-start(f32[256,384]{0,1:T(8,128)S(1)} %get-tuple-element.56), channel_id=1, source_target_pairs={{0,1},{1,2},{2,3},{3,4},{4,5},{5,6},{6,7},{8,9},{9,10},{10,11},{11... | collective-permute-start | bytes 1179656 | tf_op jit(solution)/shard_map/ppermute | solution.py:14
  446.4 8.7 %copy-start.7 = (f32[512,384]{0,1:T(8,128)}, f32[512,384]{0,1:T(8,128)S(1)}, u32[]{:S(2)}) copy-start(f32[512,384]{0,1:T(8,128)S(1)} %slice.138) | copy-start | bytes 2359300
  454.8 25.8 %copy-start.24 = (f32[256,384]{0,1:T(8,128)}, f32[256,384]{0,1:T(8,128)S(1)}, u32[]{:S(2)}) copy-start(f32[256,384]{0,1:T(8,128)S(1)} %get-tuple-element.19) | copy-start | bytes 1179652
  537.3 11.8 %collective-permute-start.17 = (f32[256,384]{0,1:T(8,128)S(1)}, f32[256,384]{0,1:T(8,128)S(1)}, u32[]{:S(2)}, u32[]{:S(2)}) collective-permute-start(f32[256,384]{0,1:T(8,128)S(1)} %get-tuple-element.17), channel_id=1, source_target_pairs={{1,0},{2,1},{3,2},{4,3},{5,4},{6,5},{7,6},{9,8},{10,9},{11,10},{12... | collective-permute-start | bytes 1179656 | tf_op jit(solution)/shard_map/ppermute | solution.py:14
  549.2 12.5 %copy-start.45 = (f32[512,384]{0,1:T(8,128)S(1)}, f32[512,384]{0,1:T(8,128)}, u32[]{:S(2)}) copy-start(f32[512,384]{0,1:T(8,128)} %copy-done.44) | copy-start | bytes 2359300
  549.5 11.9 %collective-permute-start.16 = (f32[256,384]{0,1:T(8,128)S(1)}, f32[256,384]{0,1:T(8,128)S(1)}, u32[]{:S(2)}, u32[]{:S(2)}) collective-permute-start(f32[256,384]{0,1:T(8,128)S(1)} %get-tuple-element.54), channel_id=1, source_target_pairs={{0,1},{1,2},{2,3},{3,4},{4,5},{5,6},{6,7},{8,9},{9,10},{10,11},{11... | collective-permute-start | bytes 1179656 | tf_op jit(solution)/shard_map/ppermute | solution.py:14
  552.5 9.2 %copy-start.32 = (f32[256,384]{0,1:T(8,128)S(1)}, f32[256,384]{0,1:T(8,128)}, u32[]{:S(2)}) copy-start(f32[256,384]{0,1:T(8,128)} %copy-done.30) | copy-start | bytes 1179652
  552.5 9.2 %copy-start.35 = (f32[256,384]{0,1:T(8,128)S(1)}, f32[256,384]{0,1:T(8,128)}, u32[]{:S(2)}) copy-start(f32[256,384]{0,1:T(8,128)} %copy-done.33) | copy-start | bytes 1179652
  552.5 9.2 %copy-start.37 = (f32[256,384]{0,1:T(8,128)S(1)}, f32[256,384]{0,1:T(8,128)}, u32[]{:S(2)}) copy-start(f32[256,384]{0,1:T(8,128)} %copy-done.36) | copy-start | bytes 1179652
  552.5 9.2 %copy-start.39 = (f32[256,384]{0,1:T(8,128)S(1)}, f32[256,384]{0,1:T(8,128)}, u32[]{:S(2)}) copy-start(f32[256,384]{0,1:T(8,128)} %copy-done.38) | copy-start | bytes 1179652
  552.5 9.2 %copy-start.43 = (f32[512,384]{0,1:T(8,128)S(1)}, f32[512,384]{0,1:T(8,128)}, u32[]{:S(2)}) copy-start(f32[512,384]{0,1:T(8,128)} %copy-done.41) | copy-start | bytes 2359300
  552.6 9.1 %copy-start.4 = (f32[1,1,1024,384]{2,3,1,0:T(8,128)S(1)}, f32[1,1,1024,384]{2,3,1,0:T(8,128)}, u32[]{:S(2)}) copy-start(f32[1,1,1024,384]{2,3,1,0:T(8,128)} %copy.14) | copy-start | bytes 4718596
  552.6 9.1 %copy-start.16 = (f32[512,384]{0,1:T(8,128)S(1)}, f32[512,384]{0,1:T(8,128)}, u32[]{:S(2)}) copy-start(f32[512,384]{0,1:T(8,128)} %copy-done.13) | copy-start | bytes 2359300
  563.0 13.8 %copy-start.6 = (f32[1024,384]{0,1:T(8,128)}, f32[1024,384]{0,1:T(8,128)S(1)}, u32[]{:S(2)}) copy-start(f32[1024,384]{0,1:T(8,128)S(1)} %bitcast_subtract_fusion) | copy-start | bytes 4718596
  563.1 10.1 %collective-permute-start.19 = (f32[256,384]{0,1:T(8,128)S(1)}, f32[256,384]{0,1:T(8,128)S(1)}, u32[]{:S(2)}, u32[]{:S(2)}) collective-permute-start(f32[256,384]{0,1:T(8,128)S(1)} %get-tuple-element.11), channel_id=1, source_target_pairs={{1,0},{2,1},{3,2},{4,3},{5,4},{6,5},{7,6},{9,8},{10,9},{11,10},{12... | collective-permute-start | bytes 1179656 | tf_op jit(solution)/shard_map/ppermute | solution.py:14
  574.3 10.9 %collective-permute-start.18 = (f32[256,384]{0,1:T(8,128)}, f32[256,384]{0,1:T(8,128)}, u32[]{:S(2)}, u32[]{:S(2)}) collective-permute-start(f32[256,384]{0,1:T(8,128)} %get-tuple-element.52), channel_id=1, source_target_pairs={{0,1},{1,2},{2,3},{3,4},{4,5},{5,6},{6,7},{8,9},{9,10},{10,11},{11... | collective-permute-start | bytes 1179656 | tf_op jit(solution)/shard_map/ppermute | solution.py:14
  (28 other events, 99.7 us)
Sparse Core Ops, SparseCore 0:
  92.3 35.5 all-reduce.5
  222.9 34.2 all-reduce.7
  352.2 34.2 all-reduce.9
  481.7 34.2 all-reduce.11
where the time goes:
time: 599 us; the launch traced here: 598 us
  waiting for transfers between devices  271 us (45%)
  blocking collectives  179 us (30%)
  starting transfers between devices  55.8 us (9%)
  matrix products  30 us (5%)
  local copies, waits for them, and re-layouts  23.2 us (4%)
  between operations  19.8 us (3%)
  other arithmetic  18.8 us (3%)
    psum x4, waiting for transfers between devices, on_device(): owned = lax.psum(owned, 'group')  138 us
    ppermute x18, waiting for transfers between devices, from_behind(): return lax.ppermute(block, axis, route)  133 us
    all_gather x4, blocking collectives, on_device(): all_terms = lax.all_gather(coarse_terms, 'sub', axis=0, tiled=True)  104 us
    all_to_all x4, blocking collectives, on_device(): lax.all_to_all(partial_vals, 'sub', split_axis=0, concat_axis=0, tiled=True)  59.6 us
    ppermute x18, starting transfers between devices, from_behind(): return lax.ppermute(block, axis, route)  49.6 us
    unnamed x108, local copies, waits for them, and re-layouts  15.7 us
    unnamed x1, blocking collectives  14.9 us
  transfers between devices with their start and end apart: 24, of which 21 were waited for; matrix products, arithmetic and copies ran while one was open for 4% of the time, Pallas kernels for 0%

commit v1 on v0

--- a/solution.py
+++ b/solution.py
@@ -104,7 +104,7 @@
             jnp.float32
         )
         owned = lax.dot_general(own_select, all_terms, (((0,), (0,)), ((), ())), precision=highest)
-        owned = lax.psum(owned, "group")
+        owned = jnp.sum(lax.all_gather(owned, "group"), axis=0)
         columns = jnp.take(coarse_inverse, dof_index, axis=1)
         partial_vals = lax.dot_general(columns, owned, (((0,), (0,)), ((), ())), precision=highest)
         partial_vals = partial_vals.reshape(-1, coarse_terms.shape[0], cases)

time: 599 us -> 503 us (0.84)
  waiting for transfers between devices: 271 us -> 142 us
  blocking collectives: 179 us -> 224 us
  between operations: 19.8 us -> 6.26 us
    psum x4 -> x0, waiting for transfers between devices: 138 us -> none  [on_device(): owned = lax.psum(owned, 'group')]
    all_gather x0 -> x4, blocking collectives: none -> 26.4 us  [on_device(): owned = jnp.sum(lax.all_gather(owned, 'group'), axis=0)]
    all_to_all x4, blocking collectives: 59.6 us -> 75.5 us  [on_device(): lax.all_to_all(partial_vals, 'sub', split_axis=0, concat_axis=0, tiled=True)]
    ppermute x18, waiting for transfers between devices: 133 us -> 142 us  [from_behind(): return lax.ppermute(block, axis, route)]
    reduce_sum x0 -> x4, other arithmetic: none -> 6.64 us  [on_device(): owned = jnp.sum(lax.all_gather(owned, 'group'), axis=0)]
    unnamed x108 -> x102, local copies, waits for them, and re-layouts: 15.7 us -> 14.2 us
  transfers between devices with their start and end apart: 24 -> 20, of which waited for: 21 -> 17; matrix products, arithmetic and copies ran while one was open for 4% -> 4% of each run, Pallas kernels for 0% -> 0%
where the time goes in v1:
time: 503 us; the launch traced here: 501 us
  blocking collectives  224 us (45%)
  waiting for transfers between devices  142 us (28%)
  starting transfers between devices  57.5 us (11%)
  matrix products  27.1 us (5%)
  other arithmetic  24.6 us (5%)
  local copies, waits for them, and re-layouts  20.7 us (4%)
  between operations  6.26 us (1%)
    ppermute x18, waiting for transfers between devices, from_behind(): return lax.ppermute(block, axis, route)  142 us
    all_gather x4, blocking collectives, on_device(): all_terms = lax.all_gather(coarse_terms, 'sub', axis=0, tiled=True)  105 us
    all_to_all x4, blocking collectives, on_device(): lax.all_to_all(partial_vals, 'sub', split_axis=0, concat_axis=0, tiled=True)  75.5 us
    ppermute x18, starting transfers between devices, from_behind(): return lax.ppermute(block, axis, route)  51.5 us
    all_gather x4, blocking collectives, on_device(): owned = jnp.sum(lax.all_gather(owned, 'group'), axis=0)  26.4 us
    unnamed x1, blocking collectives  16.7 us
    unnamed x102, local copies, waits for them, and re-layouts  14.2 us
    dot_general x4, matrix products, on_device(): correction = jnp.dot(neumann, weighted, preferred_element_type=jnp.float32)  10.6 us
  transfers between devices with their start and end apart: 20, of which 17 were waited for; matrix products, arithmetic and copies ran while one was open for 4% of the time, Pallas kernels for 0%

profile of v1, /device:TPU:16, one launch (start us, length us, event | category | flops | bytes accessed | tf_op | source)
XLA Modules:
  0.0 501.4 jit_solution(1694790833766985697)
XLA Ops:
  0.6 3.4 collective-permute-start.1
  6.6 3.0 copy.18
  13.3 4.2 collective-permute-start.3
  20.0 16.7 %all-reduce = f32[256]{0:T(256)S(1)} all-reduce(f32[256]{0:T(256)S(1)} %bitcast_dynamic-update-slice_fusion), channel_id=2, replica_groups=mesh['group'=4,'sub'=8] {'sub'}, use_global_device_ids=true, to_apply=%add | all-reduce | flops 256 | bytes 2048
  46.6 2.9 collective-permute-done.2
  51.5 27.6 %all_gather.43 = f32[256,384]{1,0:T(8,128)S(1)} all-gather(f32[32,384]{1,0:T(8,128)S(1)} %convolution_bitcast_fusion.3), channel_id=1, replica_groups=mesh['group'=4,'sub'=8] {'sub'}, dimensions={0}, use_global_device_ids=true | all-gather | bytes 442368 | tf_op jit(solution)/shard_map/all_gather | solution.py:99
  79.5 6.6 %all-gather.1 = f32[256,384]{1,0:T(8,128)} all-gather(f32[64,384]{1,0:T(8,128)S(1)} %fusion.97), channel_id=3, replica_groups=mesh['group'=4,'sub'=8] {'group'}, dimensions={0}, use_global_device_ids=true | all-gather | bytes 491520 | tf_op jit(solution)/shard_map/all_gather | solution.py:107
  89.1 18.8 %all_to_all.20 = f32[8,32,384]{2,1,0:T(8,128)} all-to-all(f32[8,32,384]{2,1,0:T(8,128)S(1)} %fusion.107), channel_id=1, replica_groups=mesh['group'=4,'sub'=8] {'sub'}, dimensions={0} | all-to-all | bytes 786432 | tf_op jit(solution)/shard_map/all_to_all | solution.py:111
  112.7 3.3 collective-permute-start.5
  116.0 9.6 %collective-permute-done.5 = f32[256,384]{0,1:T(8,128)S(1)} collective-permute-done((f32[256,384]{0,1:T(8,128)S(1)}, f32[256,384]{0,1:T(8,128)S(1)}, u32[]{:S(2)}, u32[]{:S(2)}) %collective-permute-start.5) | collective-permute-done | bytes 393248 | tf_op jit(solution)/shard_map/ppermute | solution.py:14
  125.9 3.0 collective-permute-start.4
  129.9 8.9 %collective-permute-done.4 = f32[256,384]{0,1:T(8,128)S(1)} collective-permute-done((f32[256,384]{0,1:T(8,128)S(1)}, f32[256,384]{0,1:T(8,128)S(1)}, u32[]{:S(2)}, u32[]{:S(2)}) %collective-permute-start.4) | collective-permute-done | bytes 393248 | tf_op jit(solution)/shard_map/ppermute | solution.py:14
  142.2 9.3 %collective-permute-done.7 = f32[256,384]{0,1:T(8,128)S(1)} collective-permute-done((f32[256,384]{0,1:T(8,128)S(1)}, f32[256,384]{0,1:T(8,128)S(1)}, u32[]{:S(2)}, u32[]{:S(2)}) %collective-permute-start.7) | collective-permute-done | bytes 393248 | tf_op jit(solution)/shard_map/ppermute | solution.py:14
  151.8 3.0 collective-permute-start.6
  154.9 8.2 %collective-permute-done.6 = f32[256,384]{0,1:T(8,128)S(1)} collective-permute-done((f32[256,384]{0,1:T(8,128)S(1)}, f32[256,384]{0,1:T(8,128)S(1)}, u32[]{:S(2)}, u32[]{:S(2)}) %collective-permute-start.6) | collective-permute-done | bytes 393248 | tf_op jit(solution)/shard_map/ppermute | solution.py:14
  163.7 25.8 %all_gather.46 = f32[256,384]{1,0:T(8,128)S(1)} all-gather(f32[32,384]{1,0:T(8,128)S(1)} %convolution_bitcast_fusion.2), channel_id=1, replica_groups=mesh['group'=4,'sub'=8] {'sub'}, dimensions={0}, use_global_device_ids=true | all-gather | bytes 442368 | tf_op jit(solution)/shard_map/all_gather | solution.py:99
  189.8 6.6 %all-gather.2 = f32[256,384]{1,0:T(8,128)} all-gather(f32[64,384]{1,0:T(8,128)S(1)} %fusion.95), channel_id=4, replica_groups=mesh['group'=4,'sub'=8] {'group'}, dimensions={0}, use_global_device_ids=true | all-gather | bytes 491520 | tf_op jit(solution)/shard_map/all_gather | solution.py:107
  199.4 18.9 %all_to_all.21 = f32[8,32,384]{2,1,0:T(8,128)} all-to-all(f32[8,32,384]{2,1,0:T(8,128)S(1)} %fusion.105), channel_id=1, replica_groups=mesh['group'=4,'sub'=8] {'sub'}, dimensions={0} | all-to-all | bytes 786432 | tf_op jit(solution)/shard_map/all_to_all | solution.py:111
  223.3 3.3 collective-permute-start.9
  226.6 9.5 %collective-permute-done.9 = f32[256,384]{0,1:T(8,128)S(1)} collective-permute-done((f32[256,384]{0,1:T(8,128)S(1)}, f32[256,384]{0,1:T(8,128)S(1)}, u32[]{:S(2)}, u32[]{:S(2)}) %collective-permute-start.9) | collective-permute-done | bytes 393248 | tf_op jit(solution)/shard_map/ppermute | solution.py:14
  236.4 3.2 collective-permute-start.8
  240.7 8.5 %collective-permute-done.8 = f32[256,384]{0,1:T(8,128)S(1)} collective-permute-done((f32[256,384]{0,1:T(8,128)S(1)}, f32[256,384]{0,1:T(8,128)S(1)}, u32[]{:S(2)}, u32[]{:S(2)}) %collective-permute-start.8) | collective-permute-done | bytes 393248 | tf_op jit(solution)/shard_map/ppermute | solution.py:14
  252.6 9.2 %collective-permute-done.11 = f32[256,384]{0,1:T(8,128)S(1)} collective-permute-done((f32[256,384]{0,1:T(8,128)S(1)}, f32[256,384]{0,1:T(8,128)S(1)}, u32[]{:S(2)}, u32[]{:S(2)}) %collective-permute-start.11) | collective-permute-done | bytes 393248 | tf_op jit(solution)/shard_map/ppermute | solution.py:14
  262.1 3.0 collective-permute-start.10
  265.1 8.0 %collective-permute-done.10 = f32[256,384]{0,1:T(8,128)S(1)} collective-permute-done((f32[256,384]{0,1:T(8,128)S(1)}, f32[256,384]{0,1:T(8,128)S(1)}, u32[]{:S(2)}, u32[]{:S(2)}) %collective-permute-start.10) | collective-permute-done | bytes 393248 | tf_op jit(solution)/shard_map/ppermute | solution.py:14
  273.8 26.0 %all_gather.49 = f32[256,384]{1,0:T(8,128)S(1)} all-gather(f32[32,384]{1,0:T(8,128)S(1)} %convolution_bitcast_fusion.1), channel_id=1, replica_groups=mesh['group'=4,'sub'=8] {'sub'}, dimensions={0}, use_global_device_ids=true | all-gather | bytes 442368 | tf_op jit(solution)/shard_map/all_gather | solution.py:99
  300.2 6.6 %all-gather.3 = f32[256,384]{1,0:T(8,128)} all-gather(f32[64,384]{1,0:T(8,128)S(1)} %fusion.93), channel_id=5, replica_groups=mesh['group'=4,'sub'=8] {'group'}, dimensions={0}, use_global_device_ids=true | all-gather | bytes 491520 | tf_op jit(solution)/shard_map/all_gather | solution.py:107
  309.8 18.8 %all_to_all.22 = f32[8,32,384]{2,1,0:T(8,128)} all-to-all(f32[8,32,384]{2,1,0:T(8,128)S(1)} %fusion.103), channel_id=1, replica_groups=mesh['group'=4,'sub'=8] {'sub'}, dimensions={0} | all-to-all | bytes 786432 | tf_op jit(solution)/shard_map/all_to_all | solution.py:111
  330.9 2.7 multiply_bitcast_fusion.1
  333.6 3.3 collective-permute-start.13
  336.9 9.6 %collective-permute-done.13 = f32[256,384]{0,1:T(8,128)S(1)} collective-permute-done((f32[256,384]{0,1:T(8,128)S(1)}, f32[256,384]{0,1:T(8,128)S(1)}, u32[]{:S(2)}, u32[]{:S(2)}) %collective-permute-start.13) | collective-permute-done | bytes 393248 | tf_op jit(solution)/shard_map/ppermute | solution.py:14
  346.8 3.0 collective-permute-start.12
  350.9 8.9 %collective-permute-done.12 = f32[256,384]{0,1:T(8,128)S(1)} collective-permute-done((f32[256,384]{0,1:T(8,128)S(1)}, f32[256,384]{0,1:T(8,128)S(1)}, u32[]{:S(2)}, u32[]{:S(2)}) %collective-permute-start.12) | collective-permute-done | bytes 393248 | tf_op jit(solution)/shard_map/ppermute | solution.py:14
  363.2 9.3 %collective-permute-done.15 = f32[256,384]{0,1:T(8,128)S(1)} collective-permute-done((f32[256,384]{0,1:T(8,128)S(1)}, f32[256,384]{0,1:T(8,128)S(1)}, u32[]{:S(2)}, u32[]{:S(2)}) %collective-permute-start.15) | collective-permute-done | bytes 393248 | tf_op jit(solution)/shard_map/ppermute | solution.py:14
  372.8 3.0 collective-permute-start.14
  375.9 8.1 %collective-permute-done.14 = f32[256,384]{0,1:T(8,128)S(1)} collective-permute-done((f32[256,384]{0,1:T(8,128)S(1)}, f32[256,384]{0,1:T(8,128)S(1)}, u32[]{:S(2)}, u32[]{:S(2)}) %collective-permute-start.14) | collective-permute-done | bytes 393248 | tf_op jit(solution)/shard_map/ppermute | solution.py:14
  384.7 25.8 %all_gather.52 = f32[256,384]{1,0:T(8,128)S(1)} all-gather(f32[32,384]{1,0:T(8,128)S(1)} %convolution_bitcast_fusion), channel_id=1, replica_groups=mesh['group'=4,'sub'=8] {'sub'}, dimensions={0}, use_global_device_ids=true | all-gather | bytes 442368 | tf_op jit(solution)/shard_map/all_gather | solution.py:99
  410.8 6.6 %all-gather.4 = f32[256,384]{1,0:T(8,128)} all-gather(f32[64,384]{1,0:T(8,128)S(1)} %fusion.91), channel_id=6, replica_groups=mesh['group'=4,'sub'=8] {'group'}, dimensions={0}, use_global_device_ids=true | all-gather | bytes 491520 | tf_op jit(solution)/shard_map/all_gather | solution.py:107
  420.4 18.9 %all_to_all.23 = f32[8,32,384]{2,1,0:T(8,128)} all-to-all(f32[8,32,384]{2,1,0:T(8,128)S(1)} %fusion.101), channel_id=1, replica_groups=mesh['group'=4,'sub'=8] {'sub'}, dimensions={0} | all-to-all | bytes 786432 | tf_op jit(solution)/shard_map/all_to_all | solution.py:111
  444.3 3.3 collective-permute-start.17
  447.6 9.5 %collective-permute-done.17 = f32[256,384]{0,1:T(8,128)S(1)} collective-permute-done((f32[256,384]{0,1:T(8,128)S(1)}, f32[256,384]{0,1:T(8,128)S(1)}, u32[]{:S(2)}, u32[]{:S(2)}) %collective-permute-start.17) | collective-permute-done | bytes 393248 | tf_op jit(solution)/shard_map/ppermute | solution.py:14
  457.4 3.2 collective-permute-start.16
  460.8 9.4 %collective-permute-done.16 = f32[256,384]{0,1:T(8,128)S(1)} collective-permute-done((f32[256,384]{0,1:T(8,128)S(1)}, f32[256,384]{0,1:T(8,128)S(1)}, u32[]{:S(2)}, u32[]{:S(2)}) %collective-permute-start.16) | collective-permute-done | bytes 393248 | tf_op jit(solution)/shard_map/ppermute | solution.py:14
  473.9 9.2 %collective-permute-done.19 = f32[256,384]{0,1:T(8,128)S(1)} collective-permute-done((f32[256,384]{0,1:T(8,128)S(1)}, f32[256,384]{0,1:T(8,128)S(1)}, u32[]{:S(2)}, u32[]{:S(2)}) %collective-permute-start.19) | collective-permute-done | bytes 393248 | tf_op jit(solution)/shard_map/ppermute | solution.py:14
  484.1 3.0 collective-permute-start.18
  488.8 3.0 copy.20
  491.8 3.7 collective-permute-done.18
  498.4 3.0 copy.21
  (190 shorter events, 72.9 us)
Async XLA Ops:
  0.6 9.0 %copy-start = (bf16[1,1,1024,1024]{3,2,1,0:T(8,128)(2,1)S(1)}, bf16[1,1,1024,1024]{3,2,1,0:T(8,128)(2,1)}, u32[]{:S(2)}) copy-start(bf16[1,1,1024,1024]{3,2,1,0:T(8,128)(2,1)} %param.15) | copy-start | bytes 6291460
  0.6 44.0 %collective-permute-start.1 = (f32[1,1]{1,0:T(1,128)}, f32[1,1]{1,0:T(1,128)}, u32[]{:S(2)}, u32[]{:S(2)}) collective-permute-start(f32[1,1]{1,0:T(1,128)} %param.13), channel_id=1, source_target_pairs={{1,0},{2,1},{3,2},{4,3},{5,4},{6,5},{7,6},{9,8},{10,9},{11,10},{12... | collective-permute-start | bytes 20 | tf_op jit(solution)/shard_map/ppermute | solution.py:25
  4.1 41.2 %collective-permute-start = (f32[1,1]{1,0:T(1,128)}, f32[1,1]{1,0:T(1,128)}, u32[]{:S(2)}, u32[]{:S(2)}) collective-permute-start(f32[1,1]{1,0:T(1,128)} %param.13), channel_id=1, source_target_pairs={{0,1},{1,2},{2,3},{3,4},{4,5},{5,6},{6,7},{8,9},{9,10},{10,11},{11... | collective-permute-start | bytes 20 | tf_op jit(solution)/shard_map/ppermute | solution.py:24
  13.3 24.1 %collective-permute-start.3 = (f32[256,384]{0,1:T(8,128)S(1)}, f32[256,384]{0,1:T(8,128)S(1)}, u32[]{:S(2)}, u32[]{:S(2)}) collective-permute-start(f32[256,384]{0,1:T(8,128)S(1)} %get-tuple-element.53), channel_id=1, source_target_pairs={{1,0},{2,1},{3,2},{4,3},{5,4},{6,5},{7,6},{9,8},{10,9},{11,10},{12... | collective-permute-start | bytes 1179656 | tf_op jit(solution)/shard_map/ppermute | solution.py:14
  38.6 10.9 %collective-permute-start.2 = (f32[256,384]{0,1:T(8,128)}, f32[256,384]{0,1:T(8,128)}, u32[]{:S(2)}, u32[]{:S(2)}) collective-permute-start(f32[256,384]{0,1:T(8,128)} %get-tuple-element.72), channel_id=1, source_target_pairs={{0,1},{1,2},{2,3},{3,4},{4,5},{5,6},{6,7},{8,9},{9,10},{10,11},{11... | collective-permute-start | bytes 1179656 | tf_op jit(solution)/shard_map/ppermute | solution.py:14
  51.2 28.4 %copy-start.22 = (f32[256,384]{0,1:T(8,128)}, f32[256,384]{0,1:T(8,128)S(1)}, u32[]{:S(2)}) copy-start(f32[256,384]{0,1:T(8,128)S(1)} %get-tuple-element.51) | copy-start | bytes 1179652
  112.7 12.9 %collective-permute-start.5 = (f32[256,384]{0,1:T(8,128)S(1)}, f32[256,384]{0,1:T(8,128)S(1)}, u32[]{:S(2)}, u32[]{:S(2)}) collective-permute-start(f32[256,384]{0,1:T(8,128)S(1)} %get-tuple-element.49), channel_id=1, source_target_pairs={{1,0},{2,1},{3,2},{4,3},{5,4},{6,5},{7,6},{9,8},{10,9},{11,10},{12... | collective-permute-start | bytes 1179656 | tf_op jit(solution)/shard_map/ppermute | solution.py:14
  125.9 13.0 %collective-permute-start.4 = (f32[256,384]{0,1:T(8,128)S(1)}, f32[256,384]{0,1:T(8,128)S(1)}, u32[]{:S(2)}, u32[]{:S(2)}) collective-permute-start(f32[256,384]{0,1:T(8,128)S(1)} %get-tuple-element.68), channel_id=1, source_target_pairs={{0,1},{1,2},{2,3},{3,4},{4,5},{5,6},{6,7},{8,9},{9,10},{10,11},{11... | collective-permute-start | bytes 1179656 | tf_op jit(solution)/shard_map/ppermute | solution.py:14
  129.9 10.3 %copy-start.13 = (f32[512,384]{0,1:T(8,128)}, f32[512,384]{0,1:T(8,128)S(1)}, u32[]{:S(2)}) copy-start(f32[512,384]{0,1:T(8,128)S(1)} %get-tuple-element.44) | copy-start | bytes 2359300
  129.9 9.2 %copy-start.1 = (f32[1,1,1024,384]{2,3,1,0:T(8,128)S(1)}, f32[1,1,1024,384]{2,3,1,0:T(8,128)}, u32[]{:S(2)}) copy-start(f32[1,1,1024,384]{2,3,1,0:T(8,128)} %copy.18) | copy-start | bytes 4718596
  140.3 11.2 %collective-permute-start.7 = (f32[256,384]{0,1:T(8,128)S(1)}, f32[256,384]{0,1:T(8,128)S(1)}, u32[]{:S(2)}, u32[]{:S(2)}) collective-permute-start(f32[256,384]{0,1:T(8,128)S(1)} %get-tuple-element.43), channel_id=1, source_target_pairs={{1,0},{2,1},{3,2},{4,3},{5,4},{6,5},{7,6},{9,8},{10,9},{11,10},{12... | collective-permute-start | bytes 1179656 | tf_op jit(solution)/shard_map/ppermute | solution.py:14
  151.8 11.2 %collective-permute-start.6 = (f32[256,384]{0,1:T(8,128)S(1)}, f32[256,384]{0,1:T(8,128)S(1)}, u32[]{:S(2)}, u32[]{:S(2)}) collective-permute-start(f32[256,384]{0,1:T(8,128)S(1)} %get-tuple-element.66), channel_id=1, source_target_pairs={{0,1},{1,2},{2,3},{3,4},{4,5},{5,6},{6,7},{8,9},{9,10},{10,11},{11... | collective-permute-start | bytes 1179656 | tf_op jit(solution)/shard_map/ppermute | solution.py:14
  154.9 8.8 %copy-start.9 = (f32[512,384]{0,1:T(8,128)}, f32[512,384]{0,1:T(8,128)S(1)}, u32[]{:S(2)}) copy-start(f32[512,384]{0,1:T(8,128)S(1)} %slice.126) | copy-start | bytes 2359300
  163.3 26.5 %copy-start.24 = (f32[256,384]{0,1:T(8,128)}, f32[256,384]{0,1:T(8,128)S(1)}, u32[]{:S(2)}) copy-start(f32[256,384]{0,1:T(8,128)S(1)} %get-tuple-element.41) | copy-start | bytes 1179652
  223.3 12.8 %collective-permute-start.9 = (f32[256,384]{0,1:T(8,128)S(1)}, f32[256,384]{0,1:T(8,128)S(1)}, u32[]{:S(2)}, u32[]{:S(2)}) collective-permute-start(f32[256,384]{0,1:T(8,128)S(1)} %get-tuple-element.39), channel_id=1, source_target_pairs={{1,0},{2,1},{3,2},{4,3},{5,4},{6,5},{7,6},{9,8},{10,9},{11,10},{12... | collective-permute-start | bytes 1179656 | tf_op jit(solution)/shard_map/ppermute | solution.py:14
  236.4 12.8 %collective-permute-start.8 = (f32[256,384]{0,1:T(8,128)S(1)}, f32[256,384]{0,1:T(8,128)S(1)}, u32[]{:S(2)}, u32[]{:S(2)}) collective-permute-start(f32[256,384]{0,1:T(8,128)S(1)} %get-tuple-element.64), channel_id=1, source_target_pairs={{0,1},{1,2},{2,3},{3,4},{4,5},{5,6},{6,7},{8,9},{9,10},{10,11},{11... | collective-permute-start | bytes 1179656 | tf_op jit(solution)/shard_map/ppermute | solution.py:14
  240.7 9.9 %copy-start.39 = (f32[512,384]{0,1:T(8,128)}, f32[512,384]{0,1:T(8,128)S(1)}, u32[]{:S(2)}) copy-start(f32[512,384]{0,1:T(8,128)S(1)} %get-tuple-element.34) | copy-start | bytes 2359300
  240.7 8.8 %copy-start.2 = (f32[1,1,1024,384]{2,3,1,0:T(8,128)S(1)}, f32[1,1,1024,384]{2,3,1,0:T(8,128)}, u32[]{:S(2)}) copy-start(f32[1,1,1024,384]{2,3,1,0:T(8,128)} %copy.18) | copy-start | bytes 4718596
  240.7 8.8 %copy-start.14 = (f32[512,384]{0,1:T(8,128)S(1)}, f32[512,384]{0,1:T(8,128)}, u32[]{:S(2)}) copy-start(f32[512,384]{0,1:T(8,128)} %copy-done.13) | copy-start | bytes 2359300
  250.7 11.1 %collective-permute-start.11 = (f32[256,384]{0,1:T(8,128)S(1)}, f32[256,384]{0,1:T(8,128)S(1)}, u32[]{:S(2)}, u32[]{:S(2)}) collective-permute-start(f32[256,384]{0,1:T(8,128)S(1)} %get-tuple-element.33), channel_id=1, source_target_pairs={{1,0},{2,1},{3,2},{4,3},{5,4},{6,5},{7,6},{9,8},{10,9},{11,10},{12... | collective-permute-start | bytes 1179656 | tf_op jit(solution)/shard_map/ppermute | solution.py:14
  262.1 11.1 %collective-permute-start.10 = (f32[256,384]{0,1:T(8,128)S(1)}, f32[256,384]{0,1:T(8,128)S(1)}, u32[]{:S(2)}, u32[]{:S(2)}) collective-permute-start(f32[256,384]{0,1:T(8,128)S(1)} %get-tuple-element.62), channel_id=1, source_target_pairs={{0,1},{1,2},{2,3},{3,4},{4,5},{5,6},{6,7},{8,9},{9,10},{10,11},{11... | collective-permute-start | bytes 1179656 | tf_op jit(solution)/shard_map/ppermute | solution.py:14
  265.1 8.7 %copy-start.11 = (f32[512,384]{0,1:T(8,128)}, f32[512,384]{0,1:T(8,128)S(1)}, u32[]{:S(2)}) copy-start(f32[512,384]{0,1:T(8,128)S(1)} %slice.132) | copy-start | bytes 2359300
  273.5 26.7 %copy-start.26 = (f32[256,384]{0,1:T(8,128)}, f32[256,384]{0,1:T(8,128)S(1)}, u32[]{:S(2)}) copy-start(f32[256,384]{0,1:T(8,128)S(1)} %get-tuple-element.31) | copy-start | bytes 1179652
  333.6 12.9 %collective-permute-start.13 = (f32[256,384]{0,1:T(8,128)S(1)}, f32[256,384]{0,1:T(8,128)S(1)}, u32[]{:S(2)}, u32[]{:S(2)}) collective-permute-start(f32[256,384]{0,1:T(8,128)S(1)} %get-tuple-element.29), channel_id=1, source_target_pairs={{1,0},{2,1},{3,2},{4,3},{5,4},{6,5},{7,6},{9,8},{10,9},{11,10},{12... | collective-permute-start | bytes 1179656 | tf_op jit(solution)/shard_map/ppermute | solution.py:14
  346.8 12.9 %collective-permute-start.12 = (f32[256,384]{0,1:T(8,128)S(1)}, f32[256,384]{0,1:T(8,128)S(1)}, u32[]{:S(2)}, u32[]{:S(2)}) collective-permute-start(f32[256,384]{0,1:T(8,128)S(1)} %get-tuple-element.60), channel_id=1, source_target_pairs={{0,1},{1,2},{2,3},{3,4},{4,5},{5,6},{6,7},{8,9},{9,10},{10,11},{11... | collective-permute-start | bytes 1179656 | tf_op jit(solution)/shard_map/ppermute | solution.py:14
  349.8 10.2 %copy-start.29 = (f32[256,384]{0,1:T(8,128)S(1)}, f32[256,384]{0,1:T(8,128)}, u32[]{:S(2)}) copy-start(f32[256,384]{0,1:T(8,128)} %copy-done.28) | copy-start | bytes 1179652
  349.8 10.2 %copy-start.32 = (f32[256,384]{0,1:T(8,128)S(1)}, f32[256,384]{0,1:T(8,128)}, u32[]{:S(2)}) copy-start(f32[256,384]{0,1:T(8,128)} %copy-done.31) | copy-start | bytes 1179652
  349.8 10.2 %copy-start.40 = (f32[512,384]{0,1:T(8,128)S(1)}, f32[512,384]{0,1:T(8,128)}, u32[]{:S(2)}) copy-start(f32[512,384]{0,1:T(8,128)} %copy-done.39) | copy-start | bytes 2359300
  350.9 10.3 %copy-start.42 = (f32[512,384]{0,1:T(8,128)}, f32[512,384]{0,1:T(8,128)S(1)}, u32[]{:S(2)}) copy-start(f32[512,384]{0,1:T(8,128)S(1)} %get-tuple-element.24) | copy-start | bytes 2359300
  350.9 9.2 %copy-start.3 = (f32[1,1,1024,384]{2,3,1,0:T(8,128)S(1)}, f32[1,1,1024,384]{2,3,1,0:T(8,128)}, u32[]{:S(2)}) copy-start(f32[1,1,1024,384]{2,3,1,0:T(8,128)} %copy.18) | copy-start | bytes 4718596
  350.9 9.2 %copy-start.15 = (f32[512,384]{0,1:T(8,128)S(1)}, f32[512,384]{0,1:T(8,128)}, u32[]{:S(2)}) copy-start(f32[512,384]{0,1:T(8,128)} %copy-done.13) | copy-start | bytes 2359300
  361.3 11.2 %collective-permute-start.15 = (f32[256,384]{0,1:T(8,128)S(1)}, f32[256,384]{0,1:T(8,128)S(1)}, u32[]{:S(2)}, u32[]{:S(2)}) collective-permute-start(f32[256,384]{0,1:T(8,128)S(1)} %get-tuple-element.23), channel_id=1, source_target_pairs={{1,0},{2,1},{3,2},{4,3},{5,4},{6,5},{7,6},{9,8},{10,9},{11,10},{12... | collective-permute-start | bytes 1179656 | tf_op jit(solution)/shard_map/ppermute | solution.py:14
  372.8 11.2 %collective-permute-start.14 = (f32[256,384]{0,1:T(8,128)S(1)}, f32[256,384]{0,1:T(8,128)S(1)}, u32[]{:S(2)}, u32[]{:S(2)}) collective-permute-start(f32[256,384]{0,1:T(8,128)S(1)} %get-tuple-element.58), channel_id=1, source_target_pairs={{0,1},{1,2},{2,3},{3,4},{4,5},{5,6},{6,7},{8,9},{9,10},{10,11},{11... | collective-permute-start | bytes 1179656 | tf_op jit(solution)/shard_map/ppermute | solution.py:14
  375.9 8.8 %copy-start.7 = (f32[512,384]{0,1:T(8,128)}, f32[512,384]{0,1:T(8,128)S(1)}, u32[]{:S(2)}) copy-start(f32[512,384]{0,1:T(8,128)S(1)} %slice.138) | copy-start | bytes 2359300
  384.3 26.5 %copy-start.20 = (f32[256,384]{0,1:T(8,128)}, f32[256,384]{0,1:T(8,128)S(1)}, u32[]{:S(2)}) copy-start(f32[256,384]{0,1:T(8,128)S(1)} %get-tuple-element.21) | copy-start | bytes 1179652
  444.3 12.8 %collective-permute-start.17 = (f32[256,384]{0,1:T(8,128)S(1)}, f32[256,384]{0,1:T(8,128)S(1)}, u32[]{:S(2)}, u32[]{:S(2)}) collective-permute-start(f32[256,384]{0,1:T(8,128)S(1)} %get-tuple-element.19), channel_id=1, source_target_pairs={{1,0},{2,1},{3,2},{4,3},{5,4},{6,5},{7,6},{9,8},{10,9},{11,10},{12... | collective-permute-start | bytes 1179656 | tf_op jit(solution)/shard_map/ppermute | solution.py:14
  457.1 13.4 %copy-start.43 = (f32[512,384]{0,1:T(8,128)S(1)}, f32[512,384]{0,1:T(8,128)}, u32[]{:S(2)}) copy-start(f32[512,384]{0,1:T(8,128)} %copy-done.42) | copy-start | bytes 2359300
  457.4 12.8 %collective-permute-start.16 = (f32[256,384]{0,1:T(8,128)S(1)}, f32[256,384]{0,1:T(8,128)S(1)}, u32[]{:S(2)}, u32[]{:S(2)}) collective-permute-start(f32[256,384]{0,1:T(8,128)S(1)} %get-tuple-element.56), channel_id=1, source_target_pairs={{0,1},{1,2},{2,3},{3,4},{4,5},{5,6},{6,7},{8,9},{9,10},{10,11},{11... | collective-permute-start | bytes 1179656 | tf_op jit(solution)/shard_map/ppermute | solution.py:14
  460.6 9.9 %copy-start.30 = (f32[256,384]{0,1:T(8,128)S(1)}, f32[256,384]{0,1:T(8,128)}, u32[]{:S(2)}) copy-start(f32[256,384]{0,1:T(8,128)} %copy-done.28) | copy-start | bytes 1179652
  460.7 9.9 %copy-start.33 = (f32[256,384]{0,1:T(8,128)S(1)}, f32[256,384]{0,1:T(8,128)}, u32[]{:S(2)}) copy-start(f32[256,384]{0,1:T(8,128)} %copy-done.31) | copy-start | bytes 1179652
  460.7 9.9 %copy-start.35 = (f32[256,384]{0,1:T(8,128)S(1)}, f32[256,384]{0,1:T(8,128)}, u32[]{:S(2)}) copy-start(f32[256,384]{0,1:T(8,128)} %copy-done.34) | copy-start | bytes 1179652
  460.7 9.9 %copy-start.37 = (f32[256,384]{0,1:T(8,128)S(1)}, f32[256,384]{0,1:T(8,128)}, u32[]{:S(2)}) copy-start(f32[256,384]{0,1:T(8,128)} %copy-done.36) | copy-start | bytes 1179652
  460.7 9.9 %copy-start.41 = (f32[512,384]{0,1:T(8,128)S(1)}, f32[512,384]{0,1:T(8,128)}, u32[]{:S(2)}) copy-start(f32[512,384]{0,1:T(8,128)} %copy-done.39) | copy-start | bytes 2359300
  460.8 9.8 %copy-start.4 = (f32[1,1,1024,384]{2,3,1,0:T(8,128)S(1)}, f32[1,1,1024,384]{2,3,1,0:T(8,128)}, u32[]{:S(2)}) copy-start(f32[1,1,1024,384]{2,3,1,0:T(8,128)} %copy.18) | copy-start | bytes 4718596
  460.8 9.8 %copy-start.16 = (f32[512,384]{0,1:T(8,128)S(1)}, f32[512,384]{0,1:T(8,128)}, u32[]{:S(2)}) copy-start(f32[512,384]{0,1:T(8,128)} %copy-done.13) | copy-start | bytes 2359300
  471.9 15.2 %copy-start.6 = (f32[1024,384]{0,1:T(8,128)}, f32[1024,384]{0,1:T(8,128)S(1)}, u32[]{:S(2)}) copy-start(f32[1024,384]{0,1:T(8,128)S(1)} %bitcast_subtract_fusion) | copy-start | bytes 4718596
  471.9 11.1 %collective-permute-start.19 = (f32[256,384]{0,1:T(8,128)S(1)}, f32[256,384]{0,1:T(8,128)S(1)}, u32[]{:S(2)}, u32[]{:S(2)}) collective-permute-start(f32[256,384]{0,1:T(8,128)S(1)} %get-tuple-element.13), channel_id=1, source_target_pairs={{1,0},{2,1},{3,2},{4,3},{5,4},{6,5},{7,6},{9,8},{10,9},{11,10},{12... | collective-permute-start | bytes 1179656 | tf_op jit(solution)/shard_map/ppermute | solution.py:14
  484.1 11.4 %collective-permute-start.18 = (f32[256,384]{0,1:T(8,128)}, f32[256,384]{0,1:T(8,128)}, u32[]{:S(2)}, u32[]{:S(2)}) collective-permute-start(f32[256,384]{0,1:T(8,128)} %get-tuple-element.54), channel_id=1, source_target_pairs={{0,1},{1,2},{2,3},{3,4},{4,5},{5,6},{6,7},{8,9},{9,10},{10,11},{11... | collective-permute-start | bytes 1179656 | tf_op jit(solution)/shard_map/ppermute | solution.py:14
  (21 other events, 60.7 us)
